TPU v7x, 128 devices: a whole 4x4x4 slice. The times are simulated.
128 devices in a mesh: dp: 4 (over x), cp: 32 (over z, y, core).
Axes of the slice: x: 4, y: 4, z: 4, core: 2. Of those that a mesh axis runs over, the one named last changes fastest.
Arguments:
- tokens: bfloat16 [4, 4096, 4096], P('dp', 'cp'), may hold values from -60 to 60
- qkv_weight: bfloat16 [4096, 3072], replicated, may hold values from -0.09375 to 0.09375
- owner_slot: int32 [4, 32], P('dp', 'cp'), may hold values from 0 to 3, as said below
- slab_sequence: int32 [4, 32], replicated, may hold values from 0 to 16, as said below
- slab_order: int32 [4, 32], replicated, may hold values from 0 to 15, as said below
Outputs:
- context: bfloat16 [4, 4096, 2048], P('dp', 'cp')
Inputs may be any that keep to these rules, and one draw needn't show every extreme that they name: For every column c, the entries owner_slot[a, c] over all rows a are 0 to 3, each once. `slab_sequence`: in each row, the slabs with one sequence number carry the orders 0 to L-1, each once, L being their count; no sequence has more than 16 slabs. `slab_order`: see slab_sequence.
All inputs are finite; a program needn't handle non-finite values.
Results may differ from a plain program's by a relative error of at most 0.006.
The roundings to bfloat16 on the way count: a program that leaves them out, or rounds other values in their place, can miss the bound.
Values may be sent and summed in bfloat16 or wider, within the bound.
No kernel may reach another device: no remote copies, remote signals or barrier semaphores. Data moves between devices by JAX's collectives and lax.ppermute only.
A program may use at most 128 MiB of HBM per device.

v0:
```python
import jax
import jax.numpy as jnp
from jax import lax
from jax.sharding import PartitionSpec as P

QH = 16
KVH = 4
HD = 128
ROPE_BASE = 500000.0
NEG_FILL = -1e30


def rotate(heads, positions):
    half_dim = heads.shape[-1] // 2
    frequency = ROPE_BASE ** (-jnp.arange(half_dim, dtype=jnp.float32) * 2.0 / heads.shape[-1])
    angles = positions.astype(jnp.float32)[:, None] * frequency[None, :]
    cosine = jnp.cos(angles)[:, None, :]
    sine_part = jnp.sin(angles)[:, None, :]
    first_half = heads[..., :half_dim]
    second_half = heads[..., half_dim:]
    return jnp.concatenate(
        [
            first_half * cosine - second_half * sine_part,
            second_half * cosine + first_half * sine_part,
        ],
        axis=-1,
    )


def project(input_rows, weight, positions):
    projected = jnp.dot(input_rows, weight, preferred_element_type=jnp.float32)
    count_rows = input_rows.shape[0]
    query = rotate(projected[:, : QH * HD].reshape(count_rows, QH, HD), positions).astype(
        jnp.bfloat16
    )
    key_heads = rotate(
        projected[:, QH * HD : (QH + KVH) * HD].reshape(count_rows, KVH, HD), positions
    ).astype(jnp.bfloat16)
    value_heads = projected[:, (QH + KVH) * HD :].astype(jnp.bfloat16)
    key_value = jnp.concatenate([key_heads.reshape(count_rows, KVH * HD), value_heads], axis=1)
    return (query.reshape(count_rows, QH * HD), key_value)


def local(tokens, qkv_weight, owner_slot, slab_sequence, slab_order):
    loader_rows = tokens[0]
    local_targets = owner_slot[0]
    slab_count = local_targets.shape[0]
    tok_dev = loader_rows.shape[0]
    slab_len = tok_dev // slab_count
    groups_count = lax.axis_size("dp")
    my_row = lax.axis_index("dp")
    column = lax.axis_index("cp")
    row_slabs = slab_sequence.shape[1]
    row_tok = row_slabs * slab_len
    group_size = QH // KVH
    offsets = jnp.arange(slab_len, dtype=jnp.int32)
    destinations = jnp.arange(groups_count * slab_count, dtype=jnp.int32)
    selector = (local_targets[None, :] == destinations[:, None]).astype(jnp.bfloat16)
    own_order = lax.dynamic_slice(slab_order, (my_row, column * slab_count), (1, slab_count))[0]
    own_pos = (own_order[:, None] * slab_len + offsets[None, :]).reshape(tok_dev)
    sent_row = local_targets // slab_count
    sent_slab = column * slab_count + local_targets % slab_count
    sent_order = slab_order[sent_row, sent_slab]
    sent_pos = (sent_order[:, None] * slab_len + offsets[None, :]).reshape(tok_dev)
    query_local, key_value_local = project(loader_rows, qkv_weight, sent_pos)
    combined = jnp.concatenate([query_local, key_value_local], axis=1)
    col_width = combined.shape[1]
    packed = jnp.einsum(
        "pj,jtd->ptd",
        selector,
        combined.reshape(slab_count, slab_len, col_width),
        preferred_element_type=jnp.float32,
    )
    received = lax.all_to_all(
        packed.astype(jnp.bfloat16).reshape(groups_count * slab_count * slab_len, col_width),
        "dp",
        split_axis=0,
        concat_axis=0,
        tiled=True,
    )
    unpack_col_width = received.shape[1]
    received = jnp.sum(
        received.reshape(groups_count, tok_dev, unpack_col_width), axis=0, dtype=jnp.float32
    ).astype(jnp.bfloat16)
    query = received[:, : QH * HD]
    key_value = received[:, QH * HD :]
    row_sequence = lax.dynamic_index_in_dim(slab_sequence, my_row, 0, keepdims=False)
    row_order = lax.dynamic_index_in_dim(slab_order, my_row, 0, keepdims=False)
    code_row = (
        row_sequence[:, None] * row_tok + row_order[:, None] * slab_len + offsets[None, :]
    ).reshape(row_tok)
    query_code = lax.dynamic_slice_in_dim(code_row, column * tok_dev, tok_dev)
    seq_start = query_code - own_pos
    query_groups = query.reshape(tok_dev, KVH, group_size, HD)
    score_scale = HD ** (-0.5)

    def update(state_now, block_keys, key_code):
        row_peak, denom_sum, weighted = state_now
        block_rows = block_keys.shape[0]
        allowed = (key_code[None, :] <= query_code[:, None]) & (
            key_code[None, :] >= seq_start[:, None]
        )

        def compute(state_in):
            peak_in, denom_in, weighted_in = state_in
            key_part = block_keys[:, : KVH * HD].reshape(block_rows, KVH, HD)
            value_part = block_keys[:, KVH * HD :].reshape(block_rows, KVH, HD)
            scores = (
                jnp.einsum(
                    "tgjh,ngh->gjtn", query_groups, key_part, preferred_element_type=jnp.float32
                )
                * score_scale
            )
            scores = jnp.where(allowed, scores, NEG_FILL)
            new_peak = jnp.maximum(peak_in, jnp.max(scores, axis=-1))
            weights = jnp.where(allowed, jnp.exp(scores - new_peak[..., None]), 0.0)
            rescale = jnp.exp(peak_in - new_peak)
            denom_out = denom_in * rescale + jnp.sum(weights, axis=-1)
            product = jnp.einsum(
                "gjtn,ngh->gjth",
                weights.astype(jnp.bfloat16),
                value_part,
                preferred_element_type=jnp.float32,
            )
            return (new_peak, denom_out, weighted_in * rescale[..., None] + product)

        return lax.cond(
            jnp.any(allowed), compute, lambda state_in: state_in, (row_peak, denom_sum, weighted)
        )

    start_state = (
        jnp.full((KVH, group_size, tok_dev), NEG_FILL, jnp.float32),
        jnp.zeros((KVH, group_size, tok_dev), jnp.float32),
        jnp.zeros((KVH, group_size, tok_dev, HD), jnp.float32),
    )
    shard_rows = lax.all_gather(key_value, "cp", axis=0, tiled=True)
    count_keys = shard_rows.shape[0]
    key_code = code_row
    step_rows = 1024
    steps_count = count_keys // step_rows

    def scan_step(state_in, pieces):
        return (update(state_in, pieces[0], pieces[1]), None)

    state_out, unused = lax.scan(
        scan_step,
        start_state,
        (
            shard_rows.reshape(steps_count, step_rows, shard_rows.shape[1]),
            key_code.reshape(steps_count, step_rows),
        ),
    )
    row_peak, denom_sum, weighted = state_out
    context = (weighted / denom_sum[..., None]).transpose(2, 0, 1, 3).reshape(tok_dev, QH * HD)
    return context.astype(jnp.bfloat16)[None]


def solution(mesh):
    in_specs = (P("dp", "cp", None), P(), P("dp", "cp"), P(), P())
    out_specs = P("dp", "cp", None)
    return jax.shard_map(local, mesh=mesh, in_specs=in_specs, out_specs=out_specs, check_vma=False)
```

profile of v0, /device:TPU:9, one launch (start us, length us, event | category | flops | bytes accessed | tf_op | source)
XLA Modules:
  0.0 182.6 jit_solution(14069714040307647107)
XLA Ops:
  6.6 1.2 copy-done
  7.8 10.0 %fusion.13 = f32[128,3072]{1,0:T(8,128)S(1)} fusion(bf16[4096,3072]{1,0:T(8,128)(2,1)} %param.10, bf16[1,128,4096]{2,1,0:T(8,128)(2,1)S(1)} %copy-done), kind=kOutput, calls=%fused_computation.19 | convolution fusion | flops 3221225472 | bytes 27787264 | tf_op jit(solution)/shard_map/dot_general | solution.py:31
  22.6 40.6 %all_to_all.6 = bf16[4,128,3072]{2,1,0:T(8,128)(2,1)} all-to-all(bf16[4,128,3072]{2,1,0:T(8,128)(2,1)S(1)} %multiply_convert_fusion), channel_id=1, replica_groups=mesh['dp'=4,'cp'=32] {'dp'}, dimensions={0} | all-to-all | bytes 6291456 | tf_op jit(solution)/shard_map/all_to_all | solution.py:74
  63.2 2.5 %reduce_sum.22 = bf16[128,3072]{1,0:T(8,128)(2,1)S(1)} reduce(bf16[4,128,3072]{2,1,0:T(8,128)(2,1)} %all_to_all.6, bf16[]{:T(256)} %constant.95.clone.1), dimensions={0}, to_apply=%region_0.1 | reduce | flops 1179648 | bytes 3932162 | tf_op jit(solution)/shard_map/reduce_sum | solution.py:82
  67.6 1.4 fusion.16
  70.0 51.5 %all-gather.2.cloned.1.call-done = bf16[4096,1024]{1,0:T(8,128)(2,1)} async-done(((bf16[128,1024]{1,0:T(8,128)(2,1)}), bf16[4096,1024]{1,0:T(8,128)(2,1)}) %all-gather.2.cloned.1.call-update) | async-done | bytes 8388624 | tf_op jit(solution)/shard_map/all_gather | solution.py:136
  121.5 11.4 %copy.18 = bf16[4,1024,1024]{1,2,0:T(8,128)(2,1)} copy(bf16[4,1024,1024]{2,1,0:T(8,128)(2,1)} %bitcast.79) | data formatting | bytes 16777216 | tf_op jit(solution)/shard_map/while | solution.py:145
  133.0 40.7 %while.15 = (s32[]{:T(128)}, f32[4,4,128]{2,1,0:T(4,128)S(1)}, f32[4,4,128]{2,1,0:T(4,128)S(1)}, f32[4,4,128,128]{3,2,1,0:T(8,128)S(1)}, s32[4,1024]{1,0:T(4,128...) while((s32[]{:T(128)}, f32[4,4,128]{2,1,0:T(4,128)S(1)}, ...), condition=%wide.region_7.8_spmd, body=%wide.region_1.7_spmd.sunk | while | flops 1102057472 | bytes 38941920 | solution.py:145
  133.1 0.8 compare_and_fusion.2
  134.6 8.6 %conditional.2 = ((f32[4,4,128]{2,1,0:T(4,128)S(1)}, f32[4,4,128]{2,1,0:T(4,128)S(1)}, f32[4,4,128,128]{3,2,1,0:T(8,128)S(1)})) conditional(s32[]{:T(128)} %convert_element_type.65, (f32[4,4,128]{2,1,0:T(4,128)S(1)}, f32[4,4,128]{2,1,0:T(4,128)S(1)}, f32[4,4,128,128]{3,2,1,0:T(8,128)S(1)}) %tuple.49, (pred[128,1024]{0,1:T(8,128)(4,1)S(1)}, ...), branch_computations={%region_3.3_spmd, %region_4.6_spmd} | conditional | flops 1101533184 | bytes 38797348 | solution.py:127
  134.6 1.8 dynamic-slice_bitcast_fusion
  136.5 1.5 fusion
  138.0 2.0 %fusion.2 = f32[4,4,128]{2,1,0:T(4,128)S(1)} fusion(f32[4,1024,128,4]{2,1,3,0:T(8,128)S(1)} %get-tuple-element.158, f32[4,4,128]{2,1,0:T(4,128)S(1)} %max.3, pred[128,1024]{0,1:T(8,128)(4,1)S(1)} %get-tuple-element.79), kind=kLoop, calls=%fused_computation.4 | loop fusion | flops 10483712 | bytes 8536064 | tf_op jit(solution)/shard_map/while/body/eval_jaxpr/cond/branch_1_fun/reduce_sum | solution.py:118
  140.1 3.1 %fusion.6 = f32[4,4,128,128]{3,2,1,0:T(8,128)S(1)} fusion(bf16[1024,4,128,1]{0,2,3,1:T(8,128)(2,1)S(1)} %bitcast.77, f32[4,1024,128,4]{2,1,3,0:T(8,128)S(1)} %get-tuple-element.158, f32[4,4,128]{2,1,0:T(4,128)S(1)} %max.3, pred[128,1024]{0,1:T(8,128)(4,1)S(1)} %get-tuple-element.79, f32[4,4,128,128]{3,2,1,0:T(8,128)S(1)} %get-tuple-element.84, ...), kind=kOutput, calls=%fused_computation.8 | convolution fusion | flops 547880960 | bytes 11681792 | tf_op jit(solution)/shard_map/while/body/eval_jaxpr/cond/branch_1_fun/gjtn,ngh->gjth/dot_general | solution.py:119
  143.2 0.8 compare_and_fusion.2
  144.7 8.6 %conditional.2 = ((f32[4,4,128]{2,1,0:T(4,128)S(1)}, f32[4,4,128]{2,1,0:T(4,128)S(1)}, f32[4,4,128,128]{3,2,1,0:T(8,128)S(1)})) conditional(s32[]{:T(128)} %convert_element_type.65, (f32[4,4,128]{2,1,0:T(4,128)S(1)}, f32[4,4,128]{2,1,0:T(4,128)S(1)}, f32[4,4,128,128]{3,2,1,0:T(8,128)S(1)}) %tuple.49, (pred[128,1024]{0,1:T(8,128)(4,1)S(1)}, ...), branch_computations={%region_3.3_spmd, %region_4.6_spmd} | conditional | flops 1101533184 | bytes 38797348 | solution.py:127
  144.7 1.8 dynamic-slice_bitcast_fusion
  146.7 1.5 fusion
  148.2 2.0 %fusion.2 = f32[4,4,128]{2,1,0:T(4,128)S(1)} fusion(f32[4,1024,128,4]{2,1,3,0:T(8,128)S(1)} %get-tuple-element.158, f32[4,4,128]{2,1,0:T(4,128)S(1)} %max.3, pred[128,1024]{0,1:T(8,128)(4,1)S(1)} %get-tuple-element.79), kind=kLoop, calls=%fused_computation.4 | loop fusion | flops 10483712 | bytes 8536064 | tf_op jit(solution)/shard_map/while/body/eval_jaxpr/cond/branch_1_fun/reduce_sum | solution.py:118
  150.2 3.1 %fusion.6 = f32[4,4,128,128]{3,2,1,0:T(8,128)S(1)} fusion(bf16[1024,4,128,1]{0,2,3,1:T(8,128)(2,1)S(1)} %bitcast.77, f32[4,1024,128,4]{2,1,3,0:T(8,128)S(1)} %get-tuple-element.158, f32[4,4,128]{2,1,0:T(4,128)S(1)} %max.3, pred[128,1024]{0,1:T(8,128)(4,1)S(1)} %get-tuple-element.79, f32[4,4,128,128]{3,2,1,0:T(8,128)S(1)} %get-tuple-element.84, ...), kind=kOutput, calls=%fused_computation.8 | convolution fusion | flops 547880960 | bytes 11681792 | tf_op jit(solution)/shard_map/while/body/eval_jaxpr/cond/branch_1_fun/gjtn,ngh->gjth/dot_general | solution.py:119
  153.4 0.8 compare_and_fusion.2
  154.9 8.6 %conditional.2 = ((f32[4,4,128]{2,1,0:T(4,128)S(1)}, f32[4,4,128]{2,1,0:T(4,128)S(1)}, f32[4,4,128,128]{3,2,1,0:T(8,128)S(1)})) conditional(s32[]{:T(128)} %convert_element_type.65, (f32[4,4,128]{2,1,0:T(4,128)S(1)}, f32[4,4,128]{2,1,0:T(4,128)S(1)}, f32[4,4,128,128]{3,2,1,0:T(8,128)S(1)}) %tuple.49, (pred[128,1024]{0,1:T(8,128)(4,1)S(1)}, ...), branch_computations={%region_3.3_spmd, %region_4.6_spmd} | conditional | flops 1101533184 | bytes 38797348 | solution.py:127
  154.9 1.8 dynamic-slice_bitcast_fusion
  156.9 1.5 fusion
  158.4 2.0 %fusion.2 = f32[4,4,128]{2,1,0:T(4,128)S(1)} fusion(f32[4,1024,128,4]{2,1,3,0:T(8,128)S(1)} %get-tuple-element.158, f32[4,4,128]{2,1,0:T(4,128)S(1)} %max.3, pred[128,1024]{0,1:T(8,128)(4,1)S(1)} %get-tuple-element.79), kind=kLoop, calls=%fused_computation.4 | loop fusion | flops 10483712 | bytes 8536064 | tf_op jit(solution)/shard_map/while/body/eval_jaxpr/cond/branch_1_fun/reduce_sum | solution.py:118
  160.4 3.1 %fusion.6 = f32[4,4,128,128]{3,2,1,0:T(8,128)S(1)} fusion(bf16[1024,4,128,1]{0,2,3,1:T(8,128)(2,1)S(1)} %bitcast.77, f32[4,1024,128,4]{2,1,3,0:T(8,128)S(1)} %get-tuple-element.158, f32[4,4,128]{2,1,0:T(4,128)S(1)} %max.3, pred[128,1024]{0,1:T(8,128)(4,1)S(1)} %get-tuple-element.79, f32[4,4,128,128]{3,2,1,0:T(8,128)S(1)} %get-tuple-element.84, ...), kind=kOutput, calls=%fused_computation.8 | convolution fusion | flops 547880960 | bytes 11681792 | tf_op jit(solution)/shard_map/while/body/eval_jaxpr/cond/branch_1_fun/gjtn,ngh->gjth/dot_general | solution.py:119
  165.1 8.6 %conditional.2 = ((f32[4,4,128]{2,1,0:T(4,128)S(1)}, f32[4,4,128]{2,1,0:T(4,128)S(1)}, f32[4,4,128,128]{3,2,1,0:T(8,128)S(1)})) conditional(s32[]{:T(128)} %convert_element_type.65, (f32[4,4,128]{2,1,0:T(4,128)S(1)}, f32[4,4,128]{2,1,0:T(4,128)S(1)}, f32[4,4,128,128]{3,2,1,0:T(8,128)S(1)}) %tuple.49, (pred[128,1024]{0,1:T(8,128)(4,1)S(1)}, ...), branch_computations={%region_3.3_spmd, %region_4.6_spmd} | conditional | flops 1101533184 | bytes 38797348 | solution.py:127
  165.1 1.8 dynamic-slice_bitcast_fusion
  167.1 1.5 fusion
  168.6 2.0 %fusion.2 = f32[4,4,128]{2,1,0:T(4,128)S(1)} fusion(f32[4,1024,128,4]{2,1,3,0:T(8,128)S(1)} %get-tuple-element.158, f32[4,4,128]{2,1,0:T(4,128)S(1)} %max.3, pred[128,1024]{0,1:T(8,128)(4,1)S(1)} %get-tuple-element.79), kind=kLoop, calls=%fused_computation.4 | loop fusion | flops 10483712 | bytes 8536064 | tf_op jit(solution)/shard_map/while/body/eval_jaxpr/cond/branch_1_fun/reduce_sum | solution.py:118
  170.6 3.1 %fusion.6 = f32[4,4,128,128]{3,2,1,0:T(8,128)S(1)} fusion(bf16[1024,4,128,1]{0,2,3,1:T(8,128)(2,1)S(1)} %bitcast.77, f32[4,1024,128,4]{2,1,3,0:T(8,128)S(1)} %get-tuple-element.158, f32[4,4,128]{2,1,0:T(4,128)S(1)} %max.3, pred[128,1024]{0,1:T(8,128)(4,1)S(1)} %get-tuple-element.79, f32[4,4,128,128]{3,2,1,0:T(8,128)S(1)} %get-tuple-element.84, ...), kind=kOutput, calls=%fused_computation.8 | convolution fusion | flops 547880960 | bytes 11681792 | tf_op jit(solution)/shard_map/while/body/eval_jaxpr/cond/branch_1_fun/gjtn,ngh->gjth/dot_general | solution.py:119
  174.5 1.2 convert_element_type.54
  (62 shorter events, 8.2 us)
Async XLA Ops:
  6.5 1.2 copy-start
  6.5 115.0 %all-gather.2.cloned.1.call-start = ((), (), s32[]{:S(2)}) async-start(), calls=%async_computation.1 | async-start | bytes 8650752 | tf_op jit(solution)/shard_map/all_gather | solution.py:136
  7.8 10.8 %copy-start.2 = (s32[4,32]{1,0:T(4,128)S(1)}, s32[4,32]{1,0:T(4,128)}, u32[]{:S(2)}) copy-start(s32[4,32]{1,0:T(4,128)} %param.13) | copy-start | bytes 1540
  173.7 2.0 %copy-start.1 = (bf16[1,128,4096]{2,1,0:T(8,128)(2,1)S(1)}, bf16[1,128,4096]{2,1,0:T(8,128)(2,1)}, u32[]{:S(2)}) copy-start(bf16[1,128,4096]{2,1,0:T(8,128)(2,1)} %param.9) | copy-start | bytes 3145732
Sparse Core Ops, SparseCore 0:
  66.6 54.8 all-gather.1
where the time goes:
time: 183 us
  waiting for transfers between devices  51.6 us (28%)
  blocking collectives  40.6 us (22%)
  matrix products  28.4 us (16%)
  local copies, waits for them, and re-layouts  25.3 us (14%)
  other arithmetic  18.2 us (10%)
  between operations  15.4 us (8%)
  loops' own time  2.98 us (2%)
    all_gather x1, waiting for transfers between devices, local(): shard_rows = lax.all_gather(key_value, 'cp', axis=0, tiled=True)  51.5 us
    all_to_all x1, blocking collectives, local(): lax.all_to_all(packed.astype(jnp.bfloat16).reshape(groups_count * slab_co...  40.6 us
    dot_general x4, matrix products, compute(): jnp.einsum('gjtn,ngh->gjth', weights.astype(jnp.bfloat16), value_part, pr...  12.4 us
    while x2, local copies, waits for them, and re-layouts, local(): lax.scan(scan_step, start_state, (shard_rows.reshape(steps_count, step_ro...  11.7 us
    dot_general x1, matrix products, project(): projected = jnp.dot(input_rows, weight, preferred_element_type=jnp.float32)  9.99 us
    reduce_sum x4, other arithmetic, compute(): denom_out = denom_in * rescale + jnp.sum(weights, axis=-1)  8.07 us
    squeeze x4, local copies, waits for them, and re-layouts, local(): lax.scan(scan_step, start_state, (shard_rows.reshape(steps_count, step_ro...  7.07 us
    dot_general x4, matrix products, compute(): jnp.einsum('tgjh,ngh->gjtn', query_groups, key_part, preferred_element_ty...  5.98 us
  transfers between devices with their start and end apart: 1, of which 1 were waited for; matrix products, arithmetic and copies ran while one was open for 2% of the time, Pallas kernels for 0%

commit v1 on v0

--- a/solution.py
+++ b/solution.py
@@ -133,7 +133,9 @@
         jnp.zeros((KVH, group_size, tok_dev), jnp.float32),
         jnp.zeros((KVH, group_size, tok_dev, HD), jnp.float32),
     )
-    shard_rows = lax.all_gather(key_value, "cp", axis=0, tiled=True)
+    shard_rows = jnp.concatenate(
+        lax.all_to_all(jnp.stack([key_value] * lax.axis_size("cp")), "cp", 0, 0), axis=0
+    )
     count_keys = shard_rows.shape[0]
     key_code = code_row
     step_rows = 1024

time: 183 us -> 230 us (1.26); the launches traced: 183 us -> 227 us
  waiting for transfers between devices: 51.6 us -> 95.4 us
  between operations: 15.4 us -> 2.15 us
  starting transfers between devices: 0.01 us -> 10 us
  local copies, waits for them, and re-layouts: 25.3 us -> 29 us
    all_to_all x0 -> x1, waiting for transfers between devices: none -> 95.4 us  [local(): lax.all_to_all(jnp.stack([key_value] * lax.axis_size('cp')), 'cp', 0, 0)]
    all_gather x1 -> x0, waiting for transfers between devices: 51.5 us -> none  [local(): shard_rows = lax.all_gather(key_value, 'cp', axis=0, tiled=True)]
    all_to_all x0 -> x1, starting transfers between devices: none -> 10 us  [local(): lax.all_to_all(jnp.stack([key_value] * lax.axis_size('cp')), 'cp', 0, 0)]
    another operation x0 -> x1, local copies, waits for them, and re-layouts: none -> 4.29 us  [local(): jnp.stack([key_value] * lax.axis_size('cp'))]
  transfers between devices with their start and end apart: 1 -> 1, of which waited for: 1 -> 1; matrix products, arithmetic and copies ran while one was open for 2% -> 1% of each run, Pallas kernels for 0% -> 0%
where the time goes in v1:
time: 230 us; the launch traced here: 227 us
  waiting for transfers between devices  95.4 us (41%)
  blocking collectives  40.6 us (18%)
  local copies, waits for them, and re-layouts  29 us (13%)
  matrix products  28.4 us (12%)
  other arithmetic  18.2 us (8%)
  starting transfers between devices  10 us (4%)
  loops' own time  2.86 us (1%)
    all_to_all x1, waiting for transfers between devices, local(): lax.all_to_all(jnp.stack([key_value] * lax.axis_size('cp')), 'cp', 0, 0)  95.4 us
    all_to_all x1, blocking collectives, local(): lax.all_to_all(packed.astype(jnp.bfloat16).reshape(groups_count * slab_co...  40.6 us
    dot_general x4, matrix products, compute(): jnp.einsum('gjtn,ngh->gjth', weights.astype(jnp.bfloat16), value_part, pr...  12.4 us
    while x2, local copies, waits for them, and re-layouts, local(): lax.scan(scan_step, start_state, (shard_rows.reshape(steps_count, step_ro...  11.7 us
    all_to_all x1, starting transfers between devices, local(): lax.all_to_all(jnp.stack([key_value] * lax.axis_size('cp')), 'cp', 0, 0)  10 us
    dot_general x1, matrix products, project(): projected = jnp.dot(input_rows, weight, preferred_element_type=jnp.float32)  9.99 us
    reduce_sum x4, other arithmetic, compute(): denom_out = denom_in * rescale + jnp.sum(weights, axis=-1)  8.07 us
    squeeze x4, local copies, waits for them, and re-layouts, local(): lax.scan(scan_step, start_state, (shard_rows.reshape(steps_count, step_ro...  7.07 us
  transfers between devices with their start and end apart: 1, of which 1 were waited for; matrix products, arithmetic and copies ran while one was open for 1% of the time, Pallas kernels for 0%

profile of v1, /device:TPU:9, one launch (start us, length us, event | category | flops | bytes accessed | tf_op | source)
XLA Modules:
  0.0 226.6 jit_solution(10662313251106367042)
XLA Ops:
  0.0 1.2 copy-done
  1.2 10.0 %fusion.13 = f32[128,3072]{1,0:T(8,128)S(1)} fusion(bf16[4096,3072]{1,0:T(8,128)(2,1)} %param.10, bf16[1,128,4096]{2,1,0:T(8,128)(2,1)S(1)} %copy-done), kind=kOutput, calls=%fused_computation.19 | convolution fusion | flops 3221225472 | bytes 27787264 | tf_op jit(solution)/shard_map/dot_general | solution.py:31
  16.1 40.6 %all_to_all.11 = bf16[4,128,3072]{2,1,0:T(8,128)(2,1)} all-to-all(bf16[4,128,3072]{2,1,0:T(8,128)(2,1)S(1)} %multiply_convert_fusion), channel_id=1, replica_groups=mesh['dp'=4,'cp'=32] {'dp'}, dimensions={0} | all-to-all | bytes 6291456 | tf_op jit(solution)/shard_map/all_to_all | solution.py:74
  56.8 2.5 %reduce_sum.22 = bf16[128,3072]{1,0:T(8,128)(2,1)S(1)} reduce(bf16[4,128,3072]{2,1,0:T(8,128)(2,1)} %all_to_all.11, bf16[]{:T(256)} %constant.95.clone.1), dimensions={0}, to_apply=%region_0.1 | reduce | flops 1179648 | bytes 3932162 | tf_op jit(solution)/shard_map/reduce_sum | solution.py:82
  59.3 4.3 %stack.2 = bf16[32,128,1024]{2,1,0:T(8,128)(2,1)} broadcast(bf16[128,1024]{1,0:T(8,128)(2,1)S(1)} %slice.65), dimensions={1,2} | broadcast | bytes 8650752 | tf_op jit(solution)/shard_map/stack | solution.py:137
  63.6 10.0 %all-to-all-start.1 = ((bf16[32,128,1024]{2,1,0:T(8,128)(2,1)}), bf16[32,128,1024]{2,1,0:T(8,128)(2,1)}, u32[]{:S(2)}, u32[]{:S(2)}) async-start(bf16[32,128,1024]{2,1,0:T(8,128)(2,1)} %stack.2), calls=%async_computation.1 | async-start | bytes 16777216 | tf_op jit(solution)/shard_map/all_to_all | solution.py:137
  74.9 1.3 fusion.16
  77.1 95.4 %all-to-all-done.1 = bf16[32,128,1024]{2,1,0:T(8,128)(2,1)} async-done(((bf16[32,128,1024]{2,1,0:T(8,128)(2,1)}), bf16[32,128,1024]{2,1,0:T(8,128)(2,1)}, u32[]{:S(2)}, u32[]{:S(2)}) %all-to-all-start.1) | async-done | bytes 8388640 | tf_op jit(solution)/shard_map/all_to_all | solution.py:137
  172.5 11.4 %copy.25 = bf16[4,1024,1024]{1,2,0:T(8,128)(2,1)} copy(bf16[4,1024,1024]{2,1,0:T(8,128)(2,1)} %bitcast.18) | data formatting | bytes 16777216 | tf_op jit(solution)/shard_map/while | solution.py:147
  184.0 40.6 %while.15 = (s32[]{:T(128)}, f32[4,4,128]{2,1,0:T(4,128)S(1)}, f32[4,4,128]{2,1,0:T(4,128)S(1)}, f32[4,4,128,128]{3,2,1,0:T(8,128)S(1)}, s32[4,1024]{1,0:T(4,128...) while((s32[]{:T(128)}, f32[4,4,128]{2,1,0:T(4,128)S(1)}, ...), condition=%wide.region_7.8_spmd, body=%wide.region_1.7_spmd.sunk | while | flops 1102057472 | bytes 38941920 | solution.py:147
  185.5 8.6 %conditional.2 = ((f32[4,4,128]{2,1,0:T(4,128)S(1)}, f32[4,4,128]{2,1,0:T(4,128)S(1)}, f32[4,4,128,128]{3,2,1,0:T(8,128)S(1)})) conditional(s32[]{:T(128)} %convert_element_type.65, (f32[4,4,128]{2,1,0:T(4,128)S(1)}, f32[4,4,128]{2,1,0:T(4,128)S(1)}, f32[4,4,128,128]{3,2,1,0:T(8,128)S(1)}) %tuple.50, (pred[128,1024]{0,1:T(8,128)(4,1)S(1)}, ...), branch_computations={%region_3.3_spmd, %region_4.6_spmd} | conditional | flops 1101533184 | bytes 38797348 | solution.py:127
  185.6 1.8 dynamic-slice_bitcast_fusion
  187.5 1.5 fusion
  189.0 2.0 fusion.2
  191.1 3.1 %fusion.6 = f32[4,4,128,128]{3,2,1,0:T(8,128)S(1)} fusion(bf16[1024,4,128,1]{0,2,3,1:T(8,128)(2,1)S(1)} %bitcast.77, f32[4,1024,128,4]{2,1,3,0:T(8,128)S(1)} %get-tuple-element.167, f32[4,4,128]{2,1,0:T(4,128)S(1)} %max.3, pred[128,1024]{0,1:T(8,128)(4,1)S(1)} %get-tuple-element.79, f32[4,4,128,128]{3,2,1,0:T(8,128)S(1)} %get-tuple-element.84, ...), kind=kOutput, calls=%fused_computation.8 | convolution fusion | flops 547880960 | bytes 11681792 | tf_op jit(solution)/shard_map/while/body/eval_jaxpr/cond/branch_1_fun/gjtn,ngh->gjth/dot_general | solution.py:119
  195.7 8.6 %conditional.2 = ((f32[4,4,128]{2,1,0:T(4,128)S(1)}, f32[4,4,128]{2,1,0:T(4,128)S(1)}, f32[4,4,128,128]{3,2,1,0:T(8,128)S(1)})) conditional(s32[]{:T(128)} %convert_element_type.65, (f32[4,4,128]{2,1,0:T(4,128)S(1)}, f32[4,4,128]{2,1,0:T(4,128)S(1)}, f32[4,4,128,128]{3,2,1,0:T(8,128)S(1)}) %tuple.50, (pred[128,1024]{0,1:T(8,128)(4,1)S(1)}, ...), branch_computations={%region_3.3_spmd, %region_4.6_spmd} | conditional | flops 1101533184 | bytes 38797348 | solution.py:127
  195.7 1.8 dynamic-slice_bitcast_fusion
  197.7 1.5 fusion
  199.2 2.0 fusion.2
  201.2 3.1 %fusion.6 = f32[4,4,128,128]{3,2,1,0:T(8,128)S(1)} fusion(bf16[1024,4,128,1]{0,2,3,1:T(8,128)(2,1)S(1)} %bitcast.77, f32[4,1024,128,4]{2,1,3,0:T(8,128)S(1)} %get-tuple-element.167, f32[4,4,128]{2,1,0:T(4,128)S(1)} %max.3, pred[128,1024]{0,1:T(8,128)(4,1)S(1)} %get-tuple-element.79, f32[4,4,128,128]{3,2,1,0:T(8,128)S(1)} %get-tuple-element.84, ...), kind=kOutput, calls=%fused_computation.8 | convolution fusion | flops 547880960 | bytes 11681792 | tf_op jit(solution)/shard_map/while/body/eval_jaxpr/cond/branch_1_fun/gjtn,ngh->gjth/dot_general | solution.py:119
  205.8 8.6 %conditional.2 = ((f32[4,4,128]{2,1,0:T(4,128)S(1)}, f32[4,4,128]{2,1,0:T(4,128)S(1)}, f32[4,4,128,128]{3,2,1,0:T(8,128)S(1)})) conditional(s32[]{:T(128)} %convert_element_type.65, (f32[4,4,128]{2,1,0:T(4,128)S(1)}, f32[4,4,128]{2,1,0:T(4,128)S(1)}, f32[4,4,128,128]{3,2,1,0:T(8,128)S(1)}) %tuple.50, (pred[128,1024]{0,1:T(8,128)(4,1)S(1)}, ...), branch_computations={%region_3.3_spmd, %region_4.6_spmd} | conditional | flops 1101533184 | bytes 38797348 | solution.py:127
  205.9 1.8 dynamic-slice_bitcast_fusion
  207.8 1.5 fusion
  209.3 2.0 fusion.2
  211.4 3.1 %fusion.6 = f32[4,4,128,128]{3,2,1,0:T(8,128)S(1)} fusion(bf16[1024,4,128,1]{0,2,3,1:T(8,128)(2,1)S(1)} %bitcast.77, f32[4,1024,128,4]{2,1,3,0:T(8,128)S(1)} %get-tuple-element.167, f32[4,4,128]{2,1,0:T(4,128)S(1)} %max.3, pred[128,1024]{0,1:T(8,128)(4,1)S(1)} %get-tuple-element.79, f32[4,4,128,128]{3,2,1,0:T(8,128)S(1)} %get-tuple-element.84, ...), kind=kOutput, calls=%fused_computation.8 | convolution fusion | flops 547880960 | bytes 11681792 | tf_op jit(solution)/shard_map/while/body/eval_jaxpr/cond/branch_1_fun/gjtn,ngh->gjth/dot_general | solution.py:119
  214.5 0.8 compare_and_fusion.2
  216.0 8.6 %conditional.2 = ((f32[4,4,128]{2,1,0:T(4,128)S(1)}, f32[4,4,128]{2,1,0:T(4,128)S(1)}, f32[4,4,128,128]{3,2,1,0:T(8,128)S(1)})) conditional(s32[]{:T(128)} %convert_element_type.65, (f32[4,4,128]{2,1,0:T(4,128)S(1)}, f32[4,4,128]{2,1,0:T(4,128)S(1)}, f32[4,4,128,128]{3,2,1,0:T(8,128)S(1)}) %tuple.50, (pred[128,1024]{0,1:T(8,128)(4,1)S(1)}, ...), branch_computations={%region_3.3_spmd, %region_4.6_spmd} | conditional | flops 1101533184 | bytes 38797348 | solution.py:127
  216.0 1.8 dynamic-slice_bitcast_fusion
  218.0 1.5 fusion
  219.5 2.0 fusion.2
  221.5 3.1 %fusion.6 = f32[4,4,128,128]{3,2,1,0:T(8,128)S(1)} fusion(bf16[1024,4,128,1]{0,2,3,1:T(8,128)(2,1)S(1)} %bitcast.77, f32[4,1024,128,4]{2,1,3,0:T(8,128)S(1)} %get-tuple-element.167, f32[4,4,128]{2,1,0:T(4,128)S(1)} %max.3, pred[128,1024]{0,1:T(8,128)(4,1)S(1)} %get-tuple-element.79, f32[4,4,128,128]{3,2,1,0:T(8,128)S(1)} %get-tuple-element.84, ...), kind=kOutput, calls=%fused_computation.8 | convolution fusion | flops 547880960 | bytes 11681792 | tf_op jit(solution)/shard_map/while/body/eval_jaxpr/cond/branch_1_fun/gjtn,ngh->gjth/dot_general | solution.py:119
  225.4 1.2 convert_element_type.54
  (62 shorter events, 9.2 us)
Async XLA Ops:
  0.0 1.2 copy-start
  1.2 10.8 %copy-start.2 = (s32[4,32]{1,0:T(4,128)S(1)}, s32[4,32]{1,0:T(4,128)}, u32[]{:S(2)}) copy-start(s32[4,32]{1,0:T(4,128)} %param.13) | copy-start | bytes 1540
  63.6 108.9 %all-to-all-start.1 = ((bf16[32,128,1024]{2,1,0:T(8,128)(2,1)}), bf16[32,128,1024]{2,1,0:T(8,128)(2,1)}, u32[]{:S(2)}, u32[]{:S(2)}) async-start(bf16[32,128,1024]{2,1,0:T(8,128)(2,1)} %stack.2), calls=%async_computation.1 | async-start | bytes 16777216 | tf_op jit(solution)/shard_map/all_to_all | solution.py:137
  224.7 2.0 copy-start.1
